TPU v7x, 32 devices: a whole 2x2x4 slice. The times are simulated.
32 devices in a mesh: row: 16 (over z, y, x), col: 2 (over core).
Axes of the slice: x: 2, y: 2, z: 4, core: 2. Of those that a mesh axis runs over, the one named last changes fastest.
Arguments:
- tokens: bfloat16 [256, 8192], P('row', 'col'), may hold values from -6 to 6
- norm_gain: float32 [8192], P('col'), may hold values from 0.1 to 1.9
- gate_weight: bfloat16 [8192, 28672], P('col', 'row'), may hold values from -0.0625 to 0.0625
- up_weight: bfloat16 [8192, 28672], P('col', 'row'), may hold values from -0.0625 to 0.0625
- down_weight: bfloat16 [28672, 8192], P('row', 'col'), may hold values from -0.03125 to 0.03125
Outputs:
- mixed: bfloat16 [256, 8192], P('row', 'col')
All inputs are finite; a program needn't handle non-finite values.
Results may differ from a plain program's by a relative error of at most 0.0065.
Values may be sent and summed in bfloat16 or wider, within the bound.
No kernel may reach another device: no remote copies, remote signals or barrier semaphores. Data moves between devices by JAX's collectives and lax.ppermute only.
A program may use at most 128 MiB of HBM per device.

v0:
```python
import jax
import jax.numpy as jnp
from jax import lax
from jax.sharding import PartitionSpec as P

D = 8192


def gated(both, width):
    return (jax.nn.silu(both[:, :width]) * both[:, width:]).astype(jnp.bfloat16)


def on_device(tokens, norm_gain, gate_weight, up_weight, down_weight):
    widened = tokens.astype(jnp.float32)
    squares = lax.psum(jnp.sum(widened * widened, axis=1, keepdims=True), "col")
    normed = (widened * norm_gain[None, :] / jnp.sqrt(squares / D + 1e-05)).astype(jnp.bfloat16)
    width = gate_weight.shape[1]
    piece = lax.all_gather(normed, "row", axis=0, tiled=True)
    gate_part = jnp.dot(piece, gate_weight, preferred_element_type=jnp.float32)
    up_part = jnp.dot(piece, up_weight, preferred_element_type=jnp.float32)
    partial_value = jnp.concatenate([gate_part, up_part], axis=1)
    shares = lax.psum_scatter(partial_value, "col", scatter_dimension=0, tiled=True)
    hidden = lax.all_gather(gated(shares, width), "col", axis=0, tiled=True)
    mixed = lax.psum_scatter(
        jnp.dot(hidden, down_weight, preferred_element_type=jnp.float32),
        "row",
        scatter_dimension=0,
        tiled=True,
    )
    return mixed.astype(jnp.bfloat16)


def solution(mesh):
    return jax.shard_map(
        on_device,
        mesh=mesh,
        in_specs=(P("row", "col"), P("col"), P("col", "row"), P("col", "row"), P("row", "col")),
        out_specs=P("row", "col"),
        check_vma=False,
    )
```

profile of v0, /device:TPU:0, one launch (start us, length us, event | category | flops | bytes accessed | tf_op | source)
XLA Modules:
  0.0 226.8 jit_solution(5429974621964089028)
XLA Ops:
  6.5 0.0 all-gather.2.cloned.1.call-start
  6.5 1.0 fusion.3
  7.6 2.6 %psum.7 = f32[16,1]{0,1:T(1,128)S(1)} all-reduce(f32[16,1]{0,1:T(1,128)S(1)} %bitcast.9), channel_id=1, replica_groups=mesh['row'=16,'col'=2] {'col'}, use_global_device_ids=true, to_apply=%region_1.0 | all-reduce | flops 16 | bytes 128 | tf_op jit(solution)/shard_map/psum | solution.py:15
  10.2 1.7 fusion.2
  11.9 0.0 all-gather.2.cloned.1.call-update
  11.9 0.0 reduce-scatter.3.cloned.1.call-start
  11.9 63.0 %all-gather.2.cloned.1.call-done = bf16[256,4096]{1,0:T(8,128)(2,1)} async-done(((bf16[16,4096]{1,0:T(8,128)(2,1)}), bf16[256,4096]{1,0:T(8,128)(2,1)}) %all-gather.2.cloned.1.call-update) | async-done | bytes 2097168 | tf_op jit(solution)/shard_map/all_gather | solution.py:18
  75.0 0.0 copy-start
  75.0 10.6 %fusion.5 = f32[256,1792]{1,0:T(8,128)S(1)} fusion(bf16[256,4096]{1,0:T(8,128)(2,1)} %all-gather.2.cloned.1.call-done, bf16[4096,1792]{1,0:T(8,128)(2,1)} %param.8), kind=kOutput, calls=%fused_computation.10 | convolution fusion | flops 3758096384 | bytes 18612224 | tf_op jit(solution)/shard_map/dot_general | solution.py:20
  85.6 0.0 copy-done
  85.6 8.0 %fusion.4 = f32[256,1792]{1,0:T(8,128)S(1)} fusion(bf16[256,4096]{1,0:T(8,128)(2,1)S(1)} %copy-done, bf16[4096,1792]{1,0:T(8,128)(2,1)} %param.7), kind=kOutput, calls=%fused_computation.9 | convolution fusion | flops 3758096384 | bytes 18612224 | tf_op jit(solution)/shard_map/dot_general | solution.py:19
  93.6 2.3 %pad_maximum_fusion = f32[256,3584]{1,0:T(8,128)} fusion(f32[256,1792]{1,0:T(8,128)S(1)} %fusion.5, f32[256,1792]{1,0:T(8,128)S(1)} %fusion.4), kind=kLoop, calls=%fused_computation | loop fusion | flops 917504 | bytes 7340032 | tf_op jit(solution)/shard_map/concatenate | solution.py:21
  95.8 0.0 reduce-scatter.3.cloned.1.call-update
  95.9 0.0 reduce-scatter.5.cloned.1.call-start
  95.9 10.8 %reduce-scatter.3.cloned.1.call-done = f32[128,3584]{1,0:T(8,128)} async-done(((f32[256,3584]{1,0:T(8,128)}), f32[128,3584]{1,0:T(8,128)}) %reduce-scatter.3.cloned.1.call-update) | async-done | bytes 1835024 | tf_op jit(solution)/shard_map/reduce_scatter | solution.py:22
  106.7 1.7 fusion
  108.4 2.5 %all_gather.7 = bf16[256,1792]{1,0:T(8,128)(2,1)S(1)} all-gather(bf16[128,1792]{1,0:T(8,128)(2,1)S(1)} %fusion), channel_id=1, replica_groups=mesh['row'=16,'col'=2] {'col'}, dimensions={0}, use_global_device_ids=true | all-gather | bytes 1376256 | tf_op jit(solution)/shard_map/all_gather | solution.py:23
  110.9 11.1 %fusion.6 = f32[256,4096]{1,0:T(8,128)} fusion(bf16[256,1792]{1,0:T(8,128)(2,1)S(1)} %all_gather.7, bf16[1792,4096]{1,0:T(8,128)(2,1)} %param.9), kind=kOutput, calls=%fused_computation.11 | convolution fusion | flops 3758096384 | bytes 19791872 | tf_op jit(solution)/shard_map/dot_general | solution.py:25
  122.0 0.0 reduce-scatter.5.cloned.1.call-update
  122.0 96.7 %reduce-scatter.5.cloned.1.call-done = f32[16,4096]{1,0:T(8,128)} async-done(((f32[256,4096]{1,0:T(8,128)}), f32[16,4096]{1,0:T(8,128)}) %reduce-scatter.5.cloned.1.call-update) | async-done | bytes 262160 | tf_op jit(solution)/shard_map/reduce_scatter | solution.py:24
  218.7 1.6 convert_element_type.15
  (1 shorter events, 0.0 us)
Async XLA Ops:
  6.5 68.5 %all-gather.2.cloned.1.call-start = ((), (), s32[]{:S(2)}) async-start(), calls=%async_computation.2 | async-start | bytes 2228224 | tf_op jit(solution)/shard_map/all_gather | solution.py:18
  11.9 94.8 %reduce-scatter.3.cloned.1.call-start = ((), (), s32[]{:S(2)}) async-start(), calls=%async_computation.3 | async-start | bytes 5505024 | tf_op jit(solution)/shard_map/reduce_scatter | solution.py:22
  75.0 10.6 %copy-start = (bf16[256,4096]{1,0:T(8,128)(2,1)S(1)}, bf16[256,4096]{1,0:T(8,128)(2,1)}, u32[]{:S(2)}) copy-start(bf16[256,4096]{1,0:T(8,128)(2,1)} %all-gather.2.cloned.1.call-done) | copy-start | bytes 6291460
  95.9 122.8 %reduce-scatter.5.cloned.1.call-start = ((), (), s32[]{:S(2)}) async-start(), calls=%async_computation.4 | async-start | bytes 4456448 | tf_op jit(solution)/shard_map/reduce_scatter | solution.py:24
Sparse Core Ops, SparseCore 0:
  12.0 62.9 all-gather.1
  96.0 10.6 reduce-scatter.2
  122.1 96.5 reduce-scatter.4
where the time goes:
time: 227 us
  waiting for transfers between devices  171 us (75%)
  matrix products  29.6 us (13%)
  between operations  13.1 us (6%)
  other arithmetic  8.33 us (4%)
  blocking collectives  5.08 us (2%)
    reduce_scatter x1, waiting for transfers between devices, on_device(): lax.psum_scatter(jnp.dot(hidden, down_weight, preferred_element_type=jnp....  96.7 us
    all_gather x1, waiting for transfers between devices, on_device(): piece = lax.all_gather(normed, 'row', axis=0, tiled=True)  63 us
    dot_general x1, matrix products, on_device(): jnp.dot(hidden, down_weight, preferred_element_type=jnp.float32)  11.1 us
    reduce_scatter x1, waiting for transfers between devices, on_device(): lax.psum_scatter(partial_value, 'col', scatter_dimension=0, tiled=True)  10.8 us
    dot_general x1, matrix products, on_device(): up_part = jnp.dot(piece, up_weight, preferred_element_type=jnp.float32)  10.6 us
    dot_general x1, matrix products, on_device(): gate_part = jnp.dot(piece, gate_weight, preferred_element_type=jnp.float32)  7.98 us
  transfers between devices with their start and end apart: 3, of which 3 were waited for; matrix products, arithmetic and copies ran while one was open for 0% of the time, Pallas kernels for 0%

commit v1 on v0

v1 whole, which is shorter than its diff:
```python
import functools

import jax
import jax.numpy as jnp
from jax import lax
from jax.experimental import pallas as pl
from jax.experimental.pallas import tpu as pltpu
from jax.sharding import PartitionSpec as P


CHUNKS = 2
PIECES = 4
F32 = jnp.float32
BF16 = jnp.bfloat16
MIB = 2**20
VMEM = pl.BlockSpec(memory_space=pltpu.VMEM)
HBM = pl.BlockSpec(memory_space=pltpu.HBM)


def size(*arrays):
    return sum(a.size * a.dtype.itemsize for a in arrays)


def call(kernel, outs, args, specs, limit, flops, out_specs=None, scratch=(), **more):
    return pl.pallas_call(
        kernel,
        out_shape=outs,
        in_specs=specs,
        out_specs=[VMEM] * len(outs) if out_specs is None else out_specs,
        scratch_shapes=scratch,
        compiler_params=pltpu.CompilerParams(vmem_limit_bytes=limit),
        cost_estimate=pl.CostEstimate(flops=flops, bytes_accessed=size(*args), transcendentals=0),
        **more,
    )(*args)


def copy_kernel(plan, *refs):
    sources, outs = refs[: len(refs) - len(plan)], refs[len(refs) - len(plan) :]
    for out, pieces in zip(outs, plan):
        at = 0
        for source, start, rows, left, lanes in pieces:
            out[pl.ds(at, rows), :] = sources[source][pl.ds(start, rows), pl.ds(left, lanes)]
            at += rows


def rearrange(sources, plan):
    shapes = [(sum(piece[2] for piece in pieces), pieces[0][4]) for pieces in plan]
    outs = [jax.ShapeDtypeStruct(shape, sources[0].dtype) for shape in shapes]
    limit = MIB + size(*sources) + size(*outs)
    return call(functools.partial(copy_kernel, plan), outs, sources, [VMEM] * len(sources), limit, 10**10)


def fetch_start(source, left, out, sems):
    pieces = sems.shape[0]
    step = out.shape[0] // pieces
    copies = [
        pltpu.make_async_copy(
            source.at[pl.ds(k * step, step), pl.ds(left, out.shape[1])], out.at[pl.ds(k * step, step), :], sems.at[k]
        )
        for k in range(pieces)
    ]
    for copy in copies:
        copy.start()
    return copies


def in_kernel(parts, left, lanes, first, last, *refs):
    tokens, refs = refs[: len(parts)], refs[len(parts) :]
    gain, weights, refs = refs[0], refs[1:3], refs[3:]
    carried, refs = (None, refs) if first else (refs[:3], refs[3:])
    down_w, refs = (refs[0], refs[1:]) if last else (None, refs)
    totals, square_out, refs = refs[:2], refs[2], refs[3:]
    sends, refs = (refs[:2], refs[2:]) if last else (None, refs)
    copies = []
    if last:
        copies, refs = fetch_start(down_w, 0, refs[0], refs[2]), refs[1:]
    scaled = refs[0]
    start = 0
    for part, offset in zip(tokens, parts):
        rows = part.shape[0]
        wide = part[:, pl.ds(offset, lanes)].astype(F32)
        scaled[pl.ds(start, rows), :] = (wide * gain[:, pl.ds(left, lanes)]).astype(BF16)
        total = None if first else carried[2][pl.ds(start, rows), :]
        for lane in range(0, lanes, 128):
            slab = wide[:, lane : lane + 128]
            total = slab * slab if total is None else total + slab * slab
        square_out[pl.ds(start, rows), :] = total
        start += rows
    for i in range(2):
        value = jnp.dot(scaled[...], weights[i][pl.ds(left, lanes), :], preferred_element_type=F32)
        if not first:
            value = value + carried[i][...]
        totals[i][...] = value
        if last:
            sends[i][...] = value.astype(BF16)
    for copy in copies:
        copy.wait()


def project_in(left, lanes, tokens, parts, gain, gate_w, up_w, carried, down_w):
    last = down_w is not None
    rows = sum(part.shape[0] for part in tokens)
    width = gate_w.shape[1]
    first = carried is None
    args = list(tokens) + [gain, gate_w, up_w] + ([] if first else list(carried))
    outs = [jax.ShapeDtypeStruct((rows, width), F32)] * 2 + [jax.ShapeDtypeStruct((rows, 128), F32)]
    specs = [VMEM] * len(args)
    if last:
        outs += [jax.ShapeDtypeStruct((rows, width), BF16)] * 2
        outs += [jax.ShapeDtypeStruct((down_w.shape[0], down_w.shape[1] // CHUNKS), BF16)]
        args += [down_w]
        specs += [HBM]
    return call(
        functools.partial(in_kernel, parts, left, lanes, first, last),
        outs,
        args,
        specs,
        6 * MIB,
        4 * rows * lanes * width,
        scratch=[
            pltpu.VMEM((rows, lanes), BF16),
            pltpu.SemaphoreType.DMA((PIECES,)),
        ],
        input_output_aliases={} if first else {len(tokens) + 3 + i: i for i in range(3)},
    )


def out_kernel(features, chunk, *refs):
    first = features is not None
    if first:
        (gate, up, square, gate_far, up_far, square_far), refs = refs[:6], refs[6:]
        near, down_w, hidden, refs = refs[0], refs[1], refs[2], refs[3:]
    else:
        (hidden, near), refs = refs[:2], refs[2:]
    send0, keep0, send1, keep1 = refs[:4]
    copies = []
    if first:
        copies = fetch_start(down_w, (chunk + 1) * near.shape[1], refs[4], refs[5])
        width = gate.shape[1]
        squares = jnp.sum(square[...] + square_far[...], axis=1, keepdims=True)
        scale = lax.rsqrt(squares / features + 1e-05)
        tile = 256 if width % 256 == 0 else width
        for lane in range(0, width, tile):
            at = pl.ds(lane, tile)
            g = (gate[:, at] + gate_far[:, at].astype(F32)) * scale
            u = (up[:, at] + up_far[:, at].astype(F32)) * scale
            hidden[:, at] = (g / (1.0 + jnp.exp(-g)) * u).astype(BF16)
    group = hidden.shape[0] // 4
    half = near.shape[1] // 2
    a = jnp.dot(hidden[...], near[:, pl.ds(0, half)], preferred_element_type=F32)
    keep0[:group] = a[:group]
    keep0[group:] = a[2 * group : 3 * group]
    send0[:group] = a[group : 2 * group].astype(BF16)
    send0[group:] = a[3 * group :].astype(BF16)
    b = jnp.dot(hidden[...], near[:, pl.ds(half, half)], preferred_element_type=F32)
    keep1[...] = b[: 2 * group]
    send1[...] = b[2 * group :].astype(BF16)
    for copy in copies:
        copy.wait()


def project_out(features, chunk, args, near, down_w):
    first = down_w is not None
    rows, depth = args[0].shape
    half = near.shape[1] // 2
    shape = lambda dtype: jax.ShapeDtypeStruct((rows // 2, half), dtype)
    outs = [shape(BF16), shape(F32), shape(BF16), shape(F32)]
    args = [*args, near]
    specs = [VMEM] * len(args)
    if first:
        args, specs = args + [down_w], specs + [HBM]
        outs = [jax.ShapeDtypeStruct((rows, depth), BF16)] + outs + [jax.ShapeDtypeStruct(near.shape, BF16)]
    return call(
        functools.partial(out_kernel, features if first else None, chunk),
        outs,
        args,
        specs,
        16 * MIB,
        4 * rows * depth * half,
        scratch=[pltpu.SemaphoreType.DMA((PIECES,))] if first else [],
    )


def solution(mesh):
    n = mesh.shape["row"]
    rest = n // 4

    def hop(value, offset):
        return lax.ppermute(value, "row", [(i, i ^ offset) for i in range(n)])

    def swap(value):
        return lax.ppermute(value, "col", [(0, 1), (1, 0)])

    def scatter(send0, keep0, send1, keep1):
        group = keep0.shape[0] // 2
        own = group // rest
        sum0 = keep0 + hop(send0, 1).astype(F32)
        sum1 = keep1 + hop(send1, 2).astype(F32)
        column0 = sum0[:group] + hop(sum0[group:].astype(BF16), 2).astype(F32)
        column1 = sum1[:group] + hop(sum1[group:].astype(BF16), 1).astype(F32)
        column = jnp.concatenate([column0, column1], axis=1)
        total = column[:own]
        for k in range(1, rest):
            total = total + hop(column[k * own : (k + 1) * own].astype(BF16), 4 * k).astype(F32)
        return total.astype(BF16)

    def on_device(tokens, norm_gain, gate_weight, up_weight, down_weight):
        features = tokens.shape[1] * mesh.shape["col"]
        gain = norm_gain[None, :]
        rows = tokens.shape[0]
        lanes = tokens.shape[1] // CHUNKS
        down_weight = pltpu.with_memory_space_constraint(down_weight, pltpu.HBM)
        mine = rearrange([tokens], [[(0, 0, rows, c * lanes, lanes)] for c in range(CHUNKS)])
        beside, above = hop(tokens, 1), hop(tokens, 2)
        columns = [[hop(mine[c], 4 * k) for k in range(1, rest)] for c in range(CHUNKS)]
        last0 = rearrange([beside], [[(0, 0, rows, 0, lanes)]])[0]
        last1 = rearrange([above], [[(0, 0, rows, lanes, lanes)]])[0]
        corner = [hop(last0, 2), hop(last1, 1)]
        carried, sends = None, None
        for c in range(CHUNKS):
            column = rearrange(columns[c], [[(k, 0, rows, 0, lanes) for k in range(rest - 1)]])[0]
            half = column.shape[0] // 2
            x, y = hop(column, 1), hop(column, 2)
            first, second = rearrange([x, y], [[(0, 0, half, 0, lanes)], [(1, half, half, 0, lanes)]])
            fy, fx = hop(first, 2), hop(second, 1)
            parts = [tokens, column, beside, x, above, y, corner[c], fy, fx]
            offsets = [c * lanes, 0, c * lanes, 0, c * lanes, 0, 0, 0, 0]
            result = project_in(c * lanes, lanes, parts, offsets, gain, gate_weight, up_weight, carried, down_weight if c == CHUNKS - 1 else None)
            carried, sends = result[:3], result[3:]
        far = [swap(sends[0]), swap(sends[1]), swap(carried[2])]
        hidden, *pieces, after = project_out(features, 0, [*carried, *far], sends[2], down_weight)
        outs = [scatter(*pieces), scatter(*project_out(None, 1, [hidden], after, None))]
        return jnp.concatenate(outs, axis=1)

    return jax.shard_map(
        on_device,
        mesh=mesh,
        in_specs=(P("row", "col"), P("col"), P("col", "row"), P("col", "row"), P("row", "col")),
        out_specs=P("row", "col"),
        check_vma=False,
    )
```

time: 227 us -> 89.1 us (0.39)
  waiting for transfers between devices: 171 us -> 29.4 us
  starting transfers between devices: 0.09 us -> 37.8 us
  matrix products: 29.6 us -> 0 us
  Pallas kernels: 0 us -> 16.9 us
  between operations: 13.1 us -> 0.35 us
  other arithmetic: 8.33 us -> 1.12 us
  blocking collectives: 5.08 us -> 0 us
  local copies, waits for them, and re-layouts: 0.01 us -> 3.33 us
    reduce_scatter x2 -> x0, waiting for transfers between devices: 107 us -> none  [the longest x1 96.7 us: on_device(): lax.psum_scatter(jnp.dot(hidden, down_weight, preferred_element_type=jnp....]
    all_gather x1 -> x0, waiting for transfers between devices: 63 us -> none  [on_device(): piece = lax.all_gather(normed, 'row', axis=0, tiled=True)]
    ppermute x0 -> x35, starting transfers between devices: none -> 37.8 us  [the longest x32 37.2 us: hop(): return lax.ppermute(value, 'row', [(i, i ^ offset) for i in range(n)])]
    dot_general x3 -> x0, matrix products: 29.6 us -> none  [the longest x1 11.1 us: on_device(): jnp.dot(hidden, down_weight, preferred_element_type=jnp.float32)]
    ppermute x0 -> x35, waiting for transfers between devices: none -> 29.4 us  [the longest x32 26 us: hop(): return lax.ppermute(value, 'row', [(i, i ^ offset) for i in range(n)])]
    pallas_call x0 -> x11, Pallas kernels: none -> 16.9 us  [call(): pl.pallas_call(kernel, out_shape=outs, in_specs=specs, out_specs=[VMEM] *...]
    convert_element_type x3 -> x2, other arithmetic: 4.99 us -> 0.07 us  [scatter(): return total.astype(BF16)]
    unnamed x2 -> x22, local copies, waits for them, and re-layouts: 0.01 us -> 3.24 us
  transfers between devices with their start and end apart: 3 -> 35, of which waited for: 3 -> 15; matrix products, arithmetic and copies ran while one was open for 0% -> 1% of each run, Pallas kernels for 0% -> 7%
where the time goes in v1:
time: 89.1 us; the launch traced here: 89 us
  starting transfers between devices  37.8 us (42%)
  waiting for transfers between devices  29.4 us (33%)
  Pallas kernels  16.9 us (19%)
  local copies, waits for them, and re-layouts  3.33 us (4%)
  other arithmetic  1.12 us (1%)
    ppermute x32, starting transfers between devices, hop(): return lax.ppermute(value, 'row', [(i, i ^ offset) for i in range(n)])  37.2 us
    ppermute x32, waiting for transfers between devices, hop(): return lax.ppermute(value, 'row', [(i, i ^ offset) for i in range(n)])  26 us
    pallas_call x11, Pallas kernels, call(): pl.pallas_call(kernel, out_shape=outs, in_specs=specs, out_specs=[VMEM] *...  16.9 us
    ppermute x3, waiting for transfers between devices, swap(): return lax.ppermute(value, 'col', [(0, 1), (1, 0)])  3.39 us
    unnamed x22, local copies, waits for them, and re-layouts  3.24 us
  transfers between devices with their start and end apart: 35, of which 15 were waited for; matrix products, arithmetic and copies ran while one was open for 1% of the time, Pallas kernels for 7%

profile of v1, /device:TPU:0, one launch (start us, length us, event | category | flops | bytes accessed | tf_op | source)
XLA Modules:
  0.0 89.0 jit_solution(6976502043717448077)
XLA Ops:
  0.9 5.1 %collective-permute-start.12 = (bf16[16,2048]{1,0:T(8,128)(2,1)S(1)}, bf16[16,2048]{1,0:T(8,128)(2,1)S(1)}, u32[]{:S(2)}, u32[]{:S(2)}) collective-permute-start(bf16[16,2048]{1,0:T(8,128)(2,1)S(1)} %get-tuple-element.33), channel_id=1, source_target_pairs={{0,24},{2,26},{4,28},{6,30},{8,16},{10,18},{12,20},{14,22},{16,8},... | collective-permute-start | bytes 196616 | tf_op jit(solution)/shard_map/ppermute | solution.py:189
  6.7 3.7 %collective-permute-start.2 = (bf16[16,2048]{1,0:T(8,128)(2,1)S(1)}, bf16[16,2048]{1,0:T(8,128)(2,1)S(1)}, u32[]{:S(2)}, u32[]{:S(2)}) collective-permute-start(bf16[16,2048]{1,0:T(8,128)(2,1)S(1)} %get-tuple-element.30), channel_id=1, source_target_pairs={{0,24},{2,26},{4,28},{6,30},{8,16},{10,18},{12,20},{14,22},{16,8},... | collective-permute-start | bytes 196616 | tf_op jit(solution)/shard_map/ppermute | solution.py:189
  11.3 3.3 %collective-permute-done.11.refs_1_ = bf16[16,2048]{1,0:T(8,128)(2,1)S(1)} collective-permute-done((bf16[16,2048]{1,0:T(8,128)(2,1)S(1)}, bf16[16,2048]{1,0:T(8,128)(2,1)S(1)}, u32[]{:S(2)}, u32[]{:S(2)}) %collective-permute-start.11) | collective-permute-done | bytes 65568 | tf_op jit(solution)/shard_map/ppermute | solution.py:189
  14.6 1.3 %collective-permute-start.5 = (bf16[16,4096]{1,0:T(8,128)(2,1)S(1)}, bf16[16,4096]{1,0:T(8,128)(2,1)S(1)}, u32[]{:S(2)}, u32[]{:S(2)}) collective-permute-start(bf16[16,4096]{1,0:T(8,128)(2,1)S(1)} %copy-done.1), channel_id=1, source_target_pairs={{0,4},{2,6},{4,0},{6,2},{8,12},{10,14},{12,8},{14,10},{16,20},{18,... | collective-permute-start | bytes 393224 | tf_op jit(solution)/shard_map/ppermute | solution.py:189
  15.9 1.5 %collective-permute-start.3 = (bf16[16,4096]{1,0:T(8,128)(2,1)S(1)}, bf16[16,4096]{1,0:T(8,128)(2,1)S(1)}, u32[]{:S(2)}, u32[]{:S(2)}) collective-permute-start(bf16[16,4096]{1,0:T(8,128)(2,1)S(1)} %copy-done.1), channel_id=1, source_target_pairs={{0,2},{2,0},{4,6},{6,4},{8,10},{10,8},{12,14},{14,12},{16,18},{18,... | collective-permute-start | bytes 393224 | tf_op jit(solution)/shard_map/ppermute | solution.py:189
  18.8 1.6 %collective-permute-start.6 = (bf16[48,2048]{1,0:T(8,128)(2,1)S(1)}, bf16[48,2048]{1,0:T(8,128)(2,1)S(1)}, u32[]{:S(2)}, u32[]{:S(2)}) collective-permute-start(bf16[48,2048]{1,0:T(8,128)(2,1)S(1)} %shard_map.56.refs_1_), channel_id=1, source_target_pairs={{0,4},{2,6},{4,0},{6,2},{8,12},{10,14},{12,8},{14,10},{16,20},{18,... | collective-permute-start | bytes 589832 | tf_op jit(solution)/shard_map/ppermute | solution.py:189
  21.0 1.3 %collective-permute-start.4 = (bf16[48,2048]{1,0:T(8,128)(2,1)S(1)}, bf16[48,2048]{1,0:T(8,128)(2,1)S(1)}, u32[]{:S(2)}, u32[]{:S(2)}) collective-permute-start(bf16[48,2048]{1,0:T(8,128)(2,1)S(1)} %shard_map.56.refs_1_), channel_id=1, source_target_pairs={{0,2},{2,0},{4,6},{6,4},{8,10},{10,8},{12,14},{14,12},{16,18},{18,... | collective-permute-start | bytes 589832 | tf_op jit(solution)/shard_map/ppermute | solution.py:189
  22.2 1.3 %collective-permute-start.7 = (bf16[16,2048]{1,0:T(8,128)(2,1)S(1)}, bf16[16,2048]{1,0:T(8,128)(2,1)S(1)}, u32[]{:S(2)}, u32[]{:S(2)}) collective-permute-start(bf16[16,2048]{1,0:T(8,128)(2,1)S(1)} %shard_map.57), channel_id=1, source_target_pairs={{0,2},{2,0},{4,6},{6,4},{8,10},{10,8},{12,14},{14,12},{16,18},{18,... | collective-permute-start | bytes 196616 | tf_op jit(solution)/shard_map/ppermute | solution.py:189
  23.6 1.7 %collective-permute-done.14.refs_1_.refs_5_ = bf16[48,2048]{1,0:T(8,128)(2,1)S(1)} collective-permute-done((bf16[48,2048]{1,0:T(8,128)(2,1)S(1)}, bf16[48,2048]{1,0:T(8,128)(2,1)S(1)}, u32[]{:S(2)}, u32[]{:S(2)}) %collective-permute-start.14) | collective-permute-done | bytes 196640 | tf_op jit(solution)/shard_map/ppermute | solution.py:189
  26.4 1.0 %collective-permute-start.16 = (bf16[24,2048]{1,0:T(8,128)(2,1)S(1)}, bf16[24,2048]{1,0:T(8,128)(2,1)S(1)}, u32[]{:S(2)}, u32[]{:S(2)}) collective-permute-start(bf16[24,2048]{1,0:T(8,128)(2,1)S(1)} %get-tuple-element.34), channel_id=1, source_target_pairs={{0,4},{2,6},{4,0},{6,2},{8,12},{10,14},{12,8},{14,10},{16,20},{18,... | collective-permute-start | bytes 294920 | tf_op jit(solution)/shard_map/ppermute | solution.py:189
  27.4 2.1 %collective-permute-done.6.refs_1_.refs_5_ = bf16[48,2048]{1,0:T(8,128)(2,1)S(1)} collective-permute-done((bf16[48,2048]{1,0:T(8,128)(2,1)S(1)}, bf16[48,2048]{1,0:T(8,128)(2,1)S(1)}, u32[]{:S(2)}, u32[]{:S(2)}) %collective-permute-start.6) | collective-permute-done | bytes 196640 | tf_op jit(solution)/shard_map/ppermute | solution.py:189
  30.6 1.0 %collective-permute-start.8 = (bf16[24,2048]{1,0:T(8,128)(2,1)S(1)}, bf16[24,2048]{1,0:T(8,128)(2,1)S(1)}, u32[]{:S(2)}, u32[]{:S(2)}) collective-permute-start(bf16[24,2048]{1,0:T(8,128)(2,1)S(1)} %get-tuple-element.31), channel_id=1, source_target_pairs={{0,4},{2,6},{4,0},{6,2},{8,12},{10,14},{12,8},{14,10},{16,20},{18,... | collective-permute-start | bytes 294920 | tf_op jit(solution)/shard_map/ppermute | solution.py:189
  32.4 1.8 %collective-permute-done.17.refs_8_ = bf16[24,2048]{1,0:T(8,128)(2,1)S(1)} collective-permute-done((bf16[24,2048]{1,0:T(8,128)(2,1)S(1)}, bf16[24,2048]{1,0:T(8,128)(2,1)S(1)}, u32[]{:S(2)}, u32[]{:S(2)}) %collective-permute-start.17) | collective-permute-done | bytes 98336 | tf_op jit(solution)/shard_map/ppermute | solution.py:189
  34.7 1.2 %slice-done.6 = s8[4194304]{0:T(1024)(128)(4,1)S(1)} async-done(((s8[14680064]{0:T(1024)(128)(4,1)}), s8[4194304]{0:T(1024)(128)(4,1)S(1)}, s32[]{:S(2)}) %slice-start.6) | async-done | bytes 4194328
  36.5 4.0 %shard_map.62 = (f32[256,1792]{1,0:T(8,128)S(1)}, f32[256,1792]{1,0:T(8,128)S(1)}, f32[256,128]{1,0:T(8,128)S(1)}) custom-call(bf16[16,4096]{1,0:T(8,128)(2,1)S(1)} %copy-done.1, bf16[48,2048]{1,0:T(8,128)(2,1)S(1)} %shard_map.59.refs_1_, bf16[16,4096]{1,0:T(8,128)(2,1)S(1)} %collective-permute-done.3.refs_0_.refs_2_, ...), custom_call_target="tpu_custom_call" | custom-call | flops 3758096384 | bytes 30621696 | tf_op jit(solution)/shard_map/pallas_call | solution.py:25
  40.5 5.7 %shard_map.63 = (f32[256,1792]{1,0:T(8,128)S(1)}, f32[256,1792]{1,0:T(8,128)S(1)}, f32[256,128]{1,0:T(8,128)S(1)}, bf16[256,1792]{1,0:T(8,128)(2,1)S(1)}, bf16[2...) custom-call(bf16[16,4096]{1,0:T(8,128)(2,1)S(1)} %copy-done.1, ...), custom_call_target="tpu_custom_call", output_to_operand_aliasing={{0}: (12, {}), {1}: (13, {}), {2}: (14, {})} | custom-call | flops 3758096384 | bytes 49102848 | tf_op jit(solution)/shard_map/pallas_call | solution.py:25
  46.9 3.4 %collective-permute-done.20.refs_5_ = f32[256,128]{1,0:T(8,128)S(1)} collective-permute-done((f32[256,128]{1,0:T(8,128)S(1)}, f32[256,128]{1,0:T(8,128)S(1)}, u32[]{:S(2)}, u32[]{:S(2)}) %collective-permute-start.20) | collective-permute-done | bytes 131104 | tf_op jit(solution)/shard_map/ppermute | solution.py:192
  50.3 5.1 %shard_map.64 = (bf16[256,1792]{1,0:T(8,128)(2,1)S(1)}, bf16[128,1024]{1,0:T(8,128)(2,1)S(1)}, f32[128,1024]{1,0:T(8,128)S(1)}, bf16[128,1024]{1,0:T(8,128)(2,1)...) custom-call(f32[256,1792]{1,0:T(8,128)S(1)} %get-tuple-element.39.refs_0_, ...), custom_call_target="tpu_custom_call" | custom-call | flops 1879048192 | bytes 27787264 | tf_op jit(solution)/shard_map/pallas_call | solution.py:25
  55.4 1.0 %collective-permute-start.21 = (bf16[128,1024]{1,0:T(8,128)(2,1)S(1)}, bf16[128,1024]{1,0:T(8,128)(2,1)S(1)}, u32[]{:S(2)}, u32[]{:S(2)}) collective-permute-start(bf16[128,1024]{1,0:T(8,128)(2,1)S(1)} %get-tuple-element.46), channel_id=1, source_target_pairs={{0,2},{2,0},{4,6},{6,4},{8,10},{10,8},{12,14},{14,12},{16,18},{18,... | collective-permute-start | bytes 786440 | tf_op jit(solution)/shard_map/ppermute | solution.py:189
  56.4 1.0 %collective-permute-start.23 = (bf16[128,1024]{1,0:T(8,128)(2,1)S(1)}, bf16[128,1024]{1,0:T(8,128)(2,1)S(1)}, u32[]{:S(2)}, u32[]{:S(2)}) collective-permute-start(bf16[128,1024]{1,0:T(8,128)(2,1)S(1)} %get-tuple-element.48), channel_id=1, source_target_pairs={{0,4},{2,6},{4,0},{6,2},{8,12},{10,14},{12,8},{14,10},{16,20},{18,... | collective-permute-start | bytes 786440 | tf_op jit(solution)/shard_map/ppermute | solution.py:189
  57.4 2.1 %shard_map.65 = (bf16[128,1024]{1,0:T(8,128)(2,1)S(1)}, f32[128,1024]{1,0:T(8,128)S(1)}, bf16[128,1024]{1,0:T(8,128)(2,1)S(1)}, f32[128,1024]{1,0:T(8,128)S(1)}) custom-call(bf16[256,1792]{1,0:T(8,128)(2,1)S(1)} %get-tuple-element.49.refs_0_, bf16[1792,2048]{1,0:T(8,128)(2,1)S(1)} %get-tuple-element.50.refs_1_), custom_call_target="tpu_custom_call" | custom-call | flops 1879048192 | bytes 8257536 | tf_op jit(solution)/shard_map/pallas_call | solution.py:25
  60.1 1.6 %collective-permute-start.30 = (bf16[128,1024]{1,0:T(8,128)(2,1)S(1)}, bf16[128,1024]{1,0:T(8,128)(2,1)S(1)}, u32[]{:S(2)}, u32[]{:S(2)}) collective-permute-start(bf16[128,1024]{1,0:T(8,128)(2,1)S(1)} %get-tuple-element.54), channel_id=1, source_target_pairs={{0,4},{2,6},{4,0},{6,2},{8,12},{10,14},{12,8},{14,10},{16,20},{18,... | collective-permute-start | bytes 786440 | tf_op jit(solution)/shard_map/ppermute | solution.py:189
  61.6 3.0 %collective-permute-done.21 = bf16[128,1024]{1,0:T(8,128)(2,1)S(1)} collective-permute-done((bf16[128,1024]{1,0:T(8,128)(2,1)S(1)}, bf16[128,1024]{1,0:T(8,128)(2,1)S(1)}, u32[]{:S(2)}, u32[]{:S(2)}) %collective-permute-start.21) | collective-permute-done | bytes 262176 | tf_op jit(solution)/shard_map/ppermute | solution.py:189
  65.6 1.2 %collective-permute-start.24 = (bf16[64,1024]{1,0:T(8,128)(2,1)S(1)}, bf16[64,1024]{1,0:T(8,128)(2,1)S(1)}, u32[]{:S(2)}, u32[]{:S(2)}) collective-permute-start(bf16[64,1024]{1,0:T(8,128)(2,1)S(1)} %slice.130), channel_id=1, source_target_pairs={{0,2},{2,0},{4,6},{6,4},{8,10},{10,8},{12,14},{14,12},{16,18},{18,... | collective-permute-start | bytes 393224 | tf_op jit(solution)/shard_map/ppermute | solution.py:189
  66.9 3.4 %collective-permute-done.28 = bf16[128,1024]{1,0:T(8,128)(2,1)S(1)} collective-permute-done((bf16[128,1024]{1,0:T(8,128)(2,1)S(1)}, bf16[128,1024]{1,0:T(8,128)(2,1)S(1)}, u32[]{:S(2)}, u32[]{:S(2)}) %collective-permute-start.28) | collective-permute-done | bytes 262176 | tf_op jit(solution)/shard_map/ppermute | solution.py:189
  71.3 1.2 %collective-permute-start.31 = (bf16[64,1024]{1,0:T(8,128)(2,1)S(1)}, bf16[64,1024]{1,0:T(8,128)(2,1)S(1)}, u32[]{:S(2)}, u32[]{:S(2)}) collective-permute-start(bf16[64,1024]{1,0:T(8,128)(2,1)S(1)} %slice.128), channel_id=1, source_target_pairs={{0,2},{2,0},{4,6},{6,4},{8,10},{10,8},{12,14},{14,12},{16,18},{18,... | collective-permute-start | bytes 393224 | tf_op jit(solution)/shard_map/ppermute | solution.py:189
  72.5 1.5 %collective-permute-done.22 = bf16[64,1024]{1,0:T(8,128)(2,1)S(1)} collective-permute-done((bf16[64,1024]{1,0:T(8,128)(2,1)S(1)}, bf16[64,1024]{1,0:T(8,128)(2,1)S(1)}, u32[]{:S(2)}, u32[]{:S(2)}) %collective-permute-start.22) | collective-permute-done | bytes 131104 | tf_op jit(solution)/shard_map/ppermute | solution.py:189
  74.2 3.1 %collective-permute-start.27 = (bf16[16,2048]{1,0:T(8,128)(2,1)S(1)}, bf16[16,2048]{1,0:T(8,128)(2,1)S(1)}, u32[]{:S(2)}, u32[]{:S(2)}) collective-permute-start(bf16[16,2048]{1,0:T(8,128)(2,1)S(1)} %get-tuple-element.56), channel_id=1, source_target_pairs={{0,24},{2,26},{4,28},{6,30},{8,16},{10,18},{12,20},{14,22},{16,8},... | collective-permute-start | bytes 196616 | tf_op jit(solution)/shard_map/ppermute | solution.py:189
  77.9 0.9 %collective-permute-start.32 = (bf16[16,2048]{1,0:T(8,128)(2,1)S(1)}, bf16[16,2048]{1,0:T(8,128)(2,1)S(1)}, u32[]{:S(2)}, u32[]{:S(2)}) collective-permute-start(bf16[16,2048]{1,0:T(8,128)(2,1)S(1)} %get-tuple-element.58), channel_id=1, source_target_pairs={{0,8},{2,10},{4,12},{6,14},{8,0},{10,2},{12,4},{14,6},{16,24},{18,... | collective-permute-start | bytes 196616 | tf_op jit(solution)/shard_map/ppermute | solution.py:189
  78.9 3.0 %collective-permute-start.34 = (bf16[16,2048]{1,0:T(8,128)(2,1)S(1)}, bf16[16,2048]{1,0:T(8,128)(2,1)S(1)}, u32[]{:S(2)}, u32[]{:S(2)}) collective-permute-start(bf16[16,2048]{1,0:T(8,128)(2,1)S(1)} %get-tuple-element.59), channel_id=1, source_target_pairs={{0,24},{2,26},{4,28},{6,30},{8,16},{10,18},{12,20},{14,22},{16,8},... | collective-permute-start | bytes 196616 | tf_op jit(solution)/shard_map/ppermute | solution.py:189
  81.9 4.0 %collective-permute-done.26 = bf16[16,2048]{1,0:T(8,128)(2,1)S(1)} collective-permute-done((bf16[16,2048]{1,0:T(8,128)(2,1)S(1)}, bf16[16,2048]{1,0:T(8,128)(2,1)S(1)}, u32[]{:S(2)}, u32[]{:S(2)}) %collective-permute-start.26) | collective-permute-done | bytes 65568 | tf_op jit(solution)/shard_map/ppermute | solution.py:189
  86.0 2.3 %collective-permute-done.33 = bf16[16,2048]{1,0:T(8,128)(2,1)S(1)} collective-permute-done((bf16[16,2048]{1,0:T(8,128)(2,1)S(1)}, bf16[16,2048]{1,0:T(8,128)(2,1)S(1)}, u32[]{:S(2)}, u32[]{:S(2)}) %collective-permute-start.33) | collective-permute-done | bytes 65568 | tf_op jit(solution)/shard_map/ppermute | solution.py:189
  (92 shorter events, 13.3 us)
Async XLA Ops:
  0.9 9.5 %collective-permute-start.12 = (bf16[16,2048]{1,0:T(8,128)(2,1)S(1)}, bf16[16,2048]{1,0:T(8,128)(2,1)S(1)}, u32[]{:S(2)}, u32[]{:S(2)}) collective-permute-start(bf16[16,2048]{1,0:T(8,128)(2,1)S(1)} %get-tuple-element.33), channel_id=1, source_target_pairs={{0,24},{2,26},{4,28},{6,30},{8,16},{10,18},{12,20},{14,22},{16,8},... | collective-permute-start | bytes 196616 | tf_op jit(solution)/shard_map/ppermute | solution.py:189
  6.1 8.5 %collective-permute-start.11 = (bf16[16,2048]{1,0:T(8,128)(2,1)S(1)}, bf16[16,2048]{1,0:T(8,128)(2,1)S(1)}, u32[]{:S(2)}, u32[]{:S(2)}) collective-permute-start(bf16[16,2048]{1,0:T(8,128)(2,1)S(1)} %get-tuple-element.33), channel_id=1, source_target_pairs={{0,16},{2,18},{4,20},{6,22},{8,24},{10,26},{12,28},{14,30},{16,0},... | collective-permute-start | bytes 196616 | tf_op jit(solution)/shard_map/ppermute | solution.py:189
  6.1 9.8 %collective-permute-start.10 = (bf16[16,2048]{1,0:T(8,128)(2,1)S(1)}, bf16[16,2048]{1,0:T(8,128)(2,1)S(1)}, u32[]{:S(2)}, u32[]{:S(2)}) collective-permute-start(bf16[16,2048]{1,0:T(8,128)(2,1)S(1)} %get-tuple-element.33), channel_id=1, source_target_pairs={{0,8},{2,10},{4,12},{6,14},{8,0},{10,2},{12,4},{14,6},{16,24},{18,... | collective-permute-start | bytes 196616 | tf_op jit(solution)/shard_map/ppermute | solution.py:189
  6.7 10.7 %collective-permute-start.2 = (bf16[16,2048]{1,0:T(8,128)(2,1)S(1)}, bf16[16,2048]{1,0:T(8,128)(2,1)S(1)}, u32[]{:S(2)}, u32[]{:S(2)}) collective-permute-start(bf16[16,2048]{1,0:T(8,128)(2,1)S(1)} %get-tuple-element.30), channel_id=1, source_target_pairs={{0,24},{2,26},{4,28},{6,30},{8,16},{10,18},{12,20},{14,22},{16,8},... | collective-permute-start | bytes 196616 | tf_op jit(solution)/shard_map/ppermute | solution.py:189
  10.5 7.5 %collective-permute-start.1 = (bf16[16,2048]{1,0:T(8,128)(2,1)S(1)}, bf16[16,2048]{1,0:T(8,128)(2,1)S(1)}, u32[]{:S(2)}, u32[]{:S(2)}) collective-permute-start(bf16[16,2048]{1,0:T(8,128)(2,1)S(1)} %get-tuple-element.30), channel_id=1, source_target_pairs={{0,16},{2,18},{4,20},{6,22},{8,24},{10,26},{12,28},{14,30},{16,0},... | collective-permute-start | bytes 196616 | tf_op jit(solution)/shard_map/ppermute | solution.py:189
  10.5 8.3 %collective-permute-start = (bf16[16,2048]{1,0:T(8,128)(2,1)S(1)}, bf16[16,2048]{1,0:T(8,128)(2,1)S(1)}, u32[]{:S(2)}, u32[]{:S(2)}) collective-permute-start(bf16[16,2048]{1,0:T(8,128)(2,1)S(1)} %get-tuple-element.30), channel_id=1, source_target_pairs={{0,8},{2,10},{4,12},{6,14},{8,0},{10,2},{12,4},{14,6},{16,24},{18,... | collective-permute-start | bytes 196616 | tf_op jit(solution)/shard_map/ppermute | solution.py:189
  14.6 6.4 %collective-permute-start.5 = (bf16[16,4096]{1,0:T(8,128)(2,1)S(1)}, bf16[16,4096]{1,0:T(8,128)(2,1)S(1)}, u32[]{:S(2)}, u32[]{:S(2)}) collective-permute-start(bf16[16,4096]{1,0:T(8,128)(2,1)S(1)} %copy-done.1), channel_id=1, source_target_pairs={{0,4},{2,6},{4,0},{6,2},{8,12},{10,14},{12,8},{14,10},{16,20},{18,... | collective-permute-start | bytes 393224 | tf_op jit(solution)/shard_map/ppermute | solution.py:189
  15.9 6.3 %collective-permute-start.3 = (bf16[16,4096]{1,0:T(8,128)(2,1)S(1)}, bf16[16,4096]{1,0:T(8,128)(2,1)S(1)}, u32[]{:S(2)}, u32[]{:S(2)}) collective-permute-start(bf16[16,4096]{1,0:T(8,128)(2,1)S(1)} %copy-done.1), channel_id=1, source_target_pairs={{0,2},{2,0},{4,6},{6,4},{8,10},{10,8},{12,14},{14,12},{16,18},{18,... | collective-permute-start | bytes 393224 | tf_op jit(solution)/shard_map/ppermute | solution.py:189
  17.4 7.8 %collective-permute-start.14 = (bf16[48,2048]{1,0:T(8,128)(2,1)S(1)}, bf16[48,2048]{1,0:T(8,128)(2,1)S(1)}, u32[]{:S(2)}, u32[]{:S(2)}) collective-permute-start(bf16[48,2048]{1,0:T(8,128)(2,1)S(1)} %shard_map.59.refs_1_), channel_id=1, source_target_pairs={{0,4},{2,6},{4,0},{6,2},{8,12},{10,14},{12,8},{14,10},{16,20},{18,... | collective-permute-start | bytes 589832 | tf_op jit(solution)/shard_map/ppermute | solution.py:189
  18.0 8.4 %collective-permute-start.13 = (bf16[48,2048]{1,0:T(8,128)(2,1)S(1)}, bf16[48,2048]{1,0:T(8,128)(2,1)S(1)}, u32[]{:S(2)}, u32[]{:S(2)}) collective-permute-start(bf16[48,2048]{1,0:T(8,128)(2,1)S(1)} %shard_map.59.refs_1_), channel_id=1, source_target_pairs={{0,2},{2,0},{4,6},{6,4},{8,10},{10,8},{12,14},{14,12},{16,18},{18,... | collective-permute-start | bytes 589832 | tf_op jit(solution)/shard_map/ppermute | solution.py:189
  18.8 10.6 %collective-permute-start.6 = (bf16[48,2048]{1,0:T(8,128)(2,1)S(1)}, bf16[48,2048]{1,0:T(8,128)(2,1)S(1)}, u32[]{:S(2)}, u32[]{:S(2)}) collective-permute-start(bf16[48,2048]{1,0:T(8,128)(2,1)S(1)} %shard_map.56.refs_1_), channel_id=1, source_target_pairs={{0,4},{2,6},{4,0},{6,2},{8,12},{10,14},{12,8},{14,10},{16,20},{18,... | collective-permute-start | bytes 589832 | tf_op jit(solution)/shard_map/ppermute | solution.py:189
  21.0 9.6 %collective-permute-start.4 = (bf16[48,2048]{1,0:T(8,128)(2,1)S(1)}, bf16[48,2048]{1,0:T(8,128)(2,1)S(1)}, u32[]{:S(2)}, u32[]{:S(2)}) collective-permute-start(bf16[48,2048]{1,0:T(8,128)(2,1)S(1)} %shard_map.56.refs_1_), channel_id=1, source_target_pairs={{0,2},{2,0},{4,6},{6,4},{8,10},{10,8},{12,14},{14,12},{16,18},{18,... | collective-permute-start | bytes 589832 | tf_op jit(solution)/shard_map/ppermute | solution.py:189
  22.2 18.3 %collective-permute-start.7 = (bf16[16,2048]{1,0:T(8,128)(2,1)S(1)}, bf16[16,2048]{1,0:T(8,128)(2,1)S(1)}, u32[]{:S(2)}, u32[]{:S(2)}) collective-permute-start(bf16[16,2048]{1,0:T(8,128)(2,1)S(1)} %shard_map.57), channel_id=1, source_target_pairs={{0,2},{2,0},{4,6},{6,4},{8,10},{10,8},{12,14},{14,12},{16,18},{18,... | collective-permute-start | bytes 196616 | tf_op jit(solution)/shard_map/ppermute | solution.py:189
  25.2 6.3 %collective-permute-start.15 = (bf16[16,2048]{1,0:T(8,128)(2,1)S(1)}, bf16[16,2048]{1,0:T(8,128)(2,1)S(1)}, u32[]{:S(2)}, u32[]{:S(2)}) collective-permute-start(bf16[16,2048]{1,0:T(8,128)(2,1)S(1)} %shard_map.60), channel_id=1, source_target_pairs={{0,4},{2,6},{4,0},{6,2},{8,12},{10,14},{12,8},{14,10},{16,20},{18,... | collective-permute-start | bytes 196616 | tf_op jit(solution)/shard_map/ppermute | solution.py:189
  26.4 6.0 %collective-permute-start.16 = (bf16[24,2048]{1,0:T(8,128)(2,1)S(1)}, bf16[24,2048]{1,0:T(8,128)(2,1)S(1)}, u32[]{:S(2)}, u32[]{:S(2)}) collective-permute-start(bf16[24,2048]{1,0:T(8,128)(2,1)S(1)} %get-tuple-element.34), channel_id=1, source_target_pairs={{0,4},{2,6},{4,0},{6,2},{8,12},{10,14},{12,8},{14,10},{16,20},{18,... | collective-permute-start | bytes 294920 | tf_op jit(solution)/shard_map/ppermute | solution.py:189
  29.5 4.7 %collective-permute-start.17 = (bf16[24,2048]{1,0:T(8,128)(2,1)S(1)}, bf16[24,2048]{1,0:T(8,128)(2,1)S(1)}, u32[]{:S(2)}, u32[]{:S(2)}) collective-permute-start(bf16[24,2048]{1,0:T(8,128)(2,1)S(1)} %get-tuple-element.35), channel_id=1, source_target_pairs={{0,2},{2,0},{4,6},{6,4},{8,10},{10,8},{12,14},{14,12},{16,18},{18,... | collective-permute-start | bytes 294920 | tf_op jit(solution)/shard_map/ppermute | solution.py:189
  30.6 9.9 %collective-permute-start.8 = (bf16[24,2048]{1,0:T(8,128)(2,1)S(1)}, bf16[24,2048]{1,0:T(8,128)(2,1)S(1)}, u32[]{:S(2)}, u32[]{:S(2)}) collective-permute-start(bf16[24,2048]{1,0:T(8,128)(2,1)S(1)} %get-tuple-element.31), channel_id=1, source_target_pairs={{0,4},{2,6},{4,0},{6,2},{8,12},{10,14},{12,8},{14,10},{16,20},{18,... | collective-permute-start | bytes 294920 | tf_op jit(solution)/shard_map/ppermute | solution.py:189
  31.6 8.9 %collective-permute-start.9 = (bf16[24,2048]{1,0:T(8,128)(2,1)S(1)}, bf16[24,2048]{1,0:T(8,128)(2,1)S(1)}, u32[]{:S(2)}, u32[]{:S(2)}) collective-permute-start(bf16[24,2048]{1,0:T(8,128)(2,1)S(1)} %get-tuple-element.32), channel_id=1, source_target_pairs={{0,2},{2,0},{4,6},{6,4},{8,10},{10,8},{12,14},{14,12},{16,18},{18,... | collective-permute-start | bytes 294920 | tf_op jit(solution)/shard_map/ppermute | solution.py:189
  55.4 9.2 %collective-permute-start.21 = (bf16[128,1024]{1,0:T(8,128)(2,1)S(1)}, bf16[128,1024]{1,0:T(8,128)(2,1)S(1)}, u32[]{:S(2)}, u32[]{:S(2)}) collective-permute-start(bf16[128,1024]{1,0:T(8,128)(2,1)S(1)} %get-tuple-element.46), channel_id=1, source_target_pairs={{0,2},{2,0},{4,6},{6,4},{8,10},{10,8},{12,14},{14,12},{16,18},{18,... | collective-permute-start | bytes 786440 | tf_op jit(solution)/shard_map/ppermute | solution.py:189
  56.4 9.2 %collective-permute-start.23 = (bf16[128,1024]{1,0:T(8,128)(2,1)S(1)}, bf16[128,1024]{1,0:T(8,128)(2,1)S(1)}, u32[]{:S(2)}, u32[]{:S(2)}) collective-permute-start(bf16[128,1024]{1,0:T(8,128)(2,1)S(1)} %get-tuple-element.48), channel_id=1, source_target_pairs={{0,4},{2,6},{4,0},{6,2},{8,12},{10,14},{12,8},{14,10},{16,20},{18,... | collective-permute-start | bytes 786440 | tf_op jit(solution)/shard_map/ppermute | solution.py:189
  59.4 10.8 %collective-permute-start.28 = (bf16[128,1024]{1,0:T(8,128)(2,1)S(1)}, bf16[128,1024]{1,0:T(8,128)(2,1)S(1)}, u32[]{:S(2)}, u32[]{:S(2)}) collective-permute-start(bf16[128,1024]{1,0:T(8,128)(2,1)S(1)} %get-tuple-element.52), channel_id=1, source_target_pairs={{0,2},{2,0},{4,6},{6,4},{8,10},{10,8},{12,14},{14,12},{16,18},{18,... | collective-permute-start | bytes 786440 | tf_op jit(solution)/shard_map/ppermute | solution.py:189
  60.1 11.1 %collective-permute-start.30 = (bf16[128,1024]{1,0:T(8,128)(2,1)S(1)}, bf16[128,1024]{1,0:T(8,128)(2,1)S(1)}, u32[]{:S(2)}, u32[]{:S(2)}) collective-permute-start(bf16[128,1024]{1,0:T(8,128)(2,1)S(1)} %get-tuple-element.54), channel_id=1, source_target_pairs={{0,4},{2,6},{4,0},{6,2},{8,12},{10,14},{12,8},{14,10},{16,20},{18,... | collective-permute-start | bytes 786440 | tf_op jit(solution)/shard_map/ppermute | solution.py:189
  64.7 9.3 %collective-permute-start.22 = (bf16[64,1024]{1,0:T(8,128)(2,1)S(1)}, bf16[64,1024]{1,0:T(8,128)(2,1)S(1)}, u32[]{:S(2)}, u32[]{:S(2)}) collective-permute-start(bf16[64,1024]{1,0:T(8,128)(2,1)S(1)} %slice.131), channel_id=1, source_target_pairs={{0,4},{2,6},{4,0},{6,2},{8,12},{10,14},{12,8},{14,10},{16,20},{18,... | collective-permute-start | bytes 393224 | tf_op jit(solution)/shard_map/ppermute | solution.py:189
  65.6 8.4 %collective-permute-start.24 = (bf16[64,1024]{1,0:T(8,128)(2,1)S(1)}, bf16[64,1024]{1,0:T(8,128)(2,1)S(1)}, u32[]{:S(2)}, u32[]{:S(2)}) collective-permute-start(bf16[64,1024]{1,0:T(8,128)(2,1)S(1)} %slice.130), channel_id=1, source_target_pairs={{0,2},{2,0},{4,6},{6,4},{8,10},{10,8},{12,14},{14,12},{16,18},{18,... | collective-permute-start | bytes 393224 | tf_op jit(solution)/shard_map/ppermute | solution.py:189
  70.3 7.5 %collective-permute-start.29 = (bf16[64,1024]{1,0:T(8,128)(2,1)S(1)}, bf16[64,1024]{1,0:T(8,128)(2,1)S(1)}, u32[]{:S(2)}, u32[]{:S(2)}) collective-permute-start(bf16[64,1024]{1,0:T(8,128)(2,1)S(1)} %slice.129), channel_id=1, source_target_pairs={{0,4},{2,6},{4,0},{6,2},{8,12},{10,14},{12,8},{14,10},{16,20},{18,... | collective-permute-start | bytes 393224 | tf_op jit(solution)/shard_map/ppermute | solution.py:189
  71.3 6.6 %collective-permute-start.31 = (bf16[64,1024]{1,0:T(8,128)(2,1)S(1)}, bf16[64,1024]{1,0:T(8,128)(2,1)S(1)}, u32[]{:S(2)}, u32[]{:S(2)}) collective-permute-start(bf16[64,1024]{1,0:T(8,128)(2,1)S(1)} %slice.128), channel_id=1, source_target_pairs={{0,2},{2,0},{4,6},{6,4},{8,10},{10,8},{12,14},{14,12},{16,18},{18,... | collective-permute-start | bytes 393224 | tf_op jit(solution)/shard_map/ppermute | solution.py:189
  74.1 7.8 %collective-permute-start.25 = (bf16[16,2048]{1,0:T(8,128)(2,1)S(1)}, bf16[16,2048]{1,0:T(8,128)(2,1)S(1)}, u32[]{:S(2)}, u32[]{:S(2)}) collective-permute-start(bf16[16,2048]{1,0:T(8,128)(2,1)S(1)} %get-tuple-element.55), channel_id=1, source_target_pairs={{0,8},{2,10},{4,12},{6,14},{8,0},{10,2},{12,4},{14,6},{16,24},{18,... | collective-permute-start | bytes 196616 | tf_op jit(solution)/shard_map/ppermute | solution.py:189
  74.2 7.7 %collective-permute-start.27 = (bf16[16,2048]{1,0:T(8,128)(2,1)S(1)}, bf16[16,2048]{1,0:T(8,128)(2,1)S(1)}, u32[]{:S(2)}, u32[]{:S(2)}) collective-permute-start(bf16[16,2048]{1,0:T(8,128)(2,1)S(1)} %get-tuple-element.56), channel_id=1, source_target_pairs={{0,24},{2,26},{4,28},{6,30},{8,16},{10,18},{12,20},{14,22},{16,8},... | collective-permute-start | bytes 196616 | tf_op jit(solution)/shard_map/ppermute | solution.py:189
  77.3 8.6 %collective-permute-start.26 = (bf16[16,2048]{1,0:T(8,128)(2,1)S(1)}, bf16[16,2048]{1,0:T(8,128)(2,1)S(1)}, u32[]{:S(2)}, u32[]{:S(2)}) collective-permute-start(bf16[16,2048]{1,0:T(8,128)(2,1)S(1)} %get-tuple-element.57), channel_id=1, source_target_pairs={{0,16},{2,18},{4,20},{6,22},{8,24},{10,26},{12,28},{14,30},{16,0},... | collective-permute-start | bytes 196616 | tf_op jit(solution)/shard_map/ppermute | solution.py:189
  77.9 8.0 %collective-permute-start.32 = (bf16[16,2048]{1,0:T(8,128)(2,1)S(1)}, bf16[16,2048]{1,0:T(8,128)(2,1)S(1)}, u32[]{:S(2)}, u32[]{:S(2)}) collective-permute-start(bf16[16,2048]{1,0:T(8,128)(2,1)S(1)} %get-tuple-element.58), channel_id=1, source_target_pairs={{0,8},{2,10},{4,12},{6,14},{8,0},{10,2},{12,4},{14,6},{16,24},{18,... | collective-permute-start | bytes 196616 | tf_op jit(solution)/shard_map/ppermute | solution.py:189
  78.9 7.1 %collective-permute-start.34 = (bf16[16,2048]{1,0:T(8,128)(2,1)S(1)}, bf16[16,2048]{1,0:T(8,128)(2,1)S(1)}, u32[]{:S(2)}, u32[]{:S(2)}) collective-permute-start(bf16[16,2048]{1,0:T(8,128)(2,1)S(1)} %get-tuple-element.59), channel_id=1, source_target_pairs={{0,24},{2,26},{4,28},{6,30},{8,16},{10,18},{12,20},{14,22},{16,8},... | collective-permute-start | bytes 196616 | tf_op jit(solution)/shard_map/ppermute | solution.py:189
  81.9 6.3 %collective-permute-start.33 = (bf16[16,2048]{1,0:T(8,128)(2,1)S(1)}, bf16[16,2048]{1,0:T(8,128)(2,1)S(1)}, u32[]{:S(2)}, u32[]{:S(2)}) collective-permute-start(bf16[16,2048]{1,0:T(8,128)(2,1)S(1)} %get-tuple-element.60), channel_id=1, source_target_pairs={{0,16},{2,18},{4,20},{6,22},{8,24},{10,26},{12,28},{14,30},{16,0},... | collective-permute-start | bytes 196616 | tf_op jit(solution)/shard_map/ppermute | solution.py:189
  (14 other events, 81.6 us)
